TPU v7x, 8 devices: a whole 2x2x1 slice. The times are simulated.
8 devices in a mesh: dp: 1 (over z), cp: 2 (over y), tp: 4 (over x, core).
Axes of the slice: x: 2, y: 2, z: 1, core: 2. Of those that a mesh axis runs over, the one named last changes fastest.
Arguments:
- x: bfloat16 [2048, 4096], P(('dp', 'cp', 'tp'))
- idx: int32 [2048, 2], P(('dp', 'cp', 'tp'))
- gates: float32 [2048, 2], P(('dp', 'cp', 'tp'))
- wq: bfloat16 [4096, 4096], P(None, 'tp')
- wk: bfloat16 [4096, 1024], P(None, 'tp')
- wv: bfloat16 [4096, 1024], P(None, 'tp')
- wo: bfloat16 [4096, 4096], P('tp')
- w1g: bfloat16 [8, 4096, 6400], P(('cp', 'tp'))
- w1u: bfloat16 [8, 4096, 6400], P(('cp', 'tp'))
- w2: bfloat16 [8, 6400, 4096], P(('cp', 'tp'))
Outputs:
- output: bfloat16 [2048, 4096], P(('dp', 'cp', 'tp'))
All inputs are finite; a program needn't handle non-finite values.
Results may differ from a plain program's by a relative error of at most 0.00893337.
Values are sent between devices in bfloat16 or wider.
A program may use at most 1 GiB of HBM per device.

v0:
```python
import jax
import jax.numpy as jnp
from jax import lax
from jax.sharding import PartitionSpec as P

HEAD_DIM = 128
NEG = -1e30


def expert_ffn(rows, wg, wu, wd):
    gg = jnp.dot(rows, wg, preferred_element_type=jnp.float32)
    uu = jnp.dot(rows, wu, preferred_element_type=jnp.float32)
    act = (jax.nn.silu(gg) * uu).astype(jnp.bfloat16)
    return jnp.dot(act, wd, preferred_element_type=jnp.float32).astype(jnp.bfloat16)


def attention_residual(x, wq, wk, wv, wo, cp):
    rank = lax.axis_index('cp')
    xs = lax.all_gather(x, 'tp', axis=0, tiled=True)
    n = xs.shape[0]
    seg = n // 2
    q = jnp.dot(xs, wq, preferred_element_type=jnp.float32).astype(jnp.bfloat16)
    k = jnp.dot(xs, wk, preferred_element_type=jnp.float32).astype(jnp.bfloat16)
    v = jnp.dot(xs, wv, preferred_element_type=jnp.float32).astype(jnp.bfloat16)
    hq = q.shape[1] // HEAD_DIM
    hkvv = k.shape[1] // HEAD_DIM
    g = hq // hkvv
    kvs = lax.all_gather(jnp.concatenate([k, v], axis=1), 'cp', axis=0)
    rows = jnp.arange(n)

    def positions(src):
        s_id = jnp.where(rows < seg, src, 2 * cp - 1 - src)
        return s_id * seg + rows % seg

    qpos = positions(rank)
    q4 = q.reshape(n, hkvv, g, HEAD_DIM)
    scale = HEAD_DIM ** -0.5
    m = jnp.full((hkvv, g, n), NEG, jnp.float32)
    l = jnp.zeros((hkvv, g, n), jnp.float32)
    acc = jnp.zeros((hkvv, g, n, HEAD_DIM), jnp.float32)
    for j in range(cp):
        kj = kvs[j, :, :hkvv * HEAD_DIM].reshape(n, hkvv, HEAD_DIM)
        vj = kvs[j, :, hkvv * HEAD_DIM:].reshape(n, hkvv, HEAD_DIM)
        mask = positions(j)[None, :] <= qpos[:, None]
        s = jnp.einsum('nkgd,mkd->kgnm', q4, kj, preferred_element_type=jnp.float32) * scale
        s = jnp.where(mask, s, NEG)
        mn = jnp.maximum(m, jnp.max(s, axis=-1))
        w = jnp.where(mask, jnp.exp(s - mn[:, :, :, None]), 0.0)
        c = jnp.exp(m - mn)
        l = l * c + jnp.sum(w, axis=-1)
        acc = acc * c[:, :, :, None] + jnp.einsum('kgnm,mkd->kgnd', w.astype(jnp.bfloat16), vj, preferred_element_type=jnp.float32)
        m = mn
    o = (acc / l[:, :, :, None]).transpose(2, 0, 1, 3).reshape(n, hq * HEAD_DIM).astype(jnp.bfloat16)
    part = jnp.dot(o, wo, preferred_element_type=jnp.float32)
    att = lax.psum_scatter(part, 'tp', scatter_dimension=0, tiled=True)
    return (x.astype(jnp.float32) + att).astype(jnp.bfloat16)


def solution(mesh):
    cp = mesh.shape['cp']
    tp = mesh.shape['tp']
    ne = cp * tp
    rows_spec = P(('dp', 'cp', 'tp'), None)
    exp_spec = P(('cp', 'tp'), None, None)

    def local(x, idx, gates, wq, wk, wv, wo, w1g, w1u, w2):
        h = attention_residual(x, wq, wk, wv, wo, cp)
        t, hd = h.shape
        kk = idx.shape[1]
        cap = 4 * t // ne
        ea = idx.reshape(-1)
        tok = jnp.arange(t * kk) // kk
        onehot = (ea[:, None] == jnp.arange(ne)[None, :]).astype(jnp.int32)
        slot = jnp.take_along_axis(jnp.cumsum(onehot, axis=0), ea[:, None], axis=1)[:, 0] - 1
        send = jnp.zeros((ne, cap, hd), jnp.bfloat16).at[ea, slot].set(h[tok])
        recv = lax.all_to_all(send, ('cp', 'tp'), 0, 0, tiled=True)
        z = expert_ffn(recv.reshape(ne * cap, hd), w1g[0], w1u[0], w2[0])
        back = lax.all_to_all(z.reshape(ne, cap, hd), ('cp', 'tp'), 0, 0, tiled=True)
        zt = back[ea, slot].astype(jnp.float32).reshape(t, kk, hd)
        y = h.astype(jnp.float32) + jnp.sum(gates[:, :, None] * zt, axis=1)
        return y.astype(jnp.bfloat16)

    return jax.shard_map(local, mesh=mesh, in_specs=(rows_spec, rows_spec, rows_spec, P(None, 'tp'), P(None, 'tp'), P(None, 'tp'), P('tp', None), exp_spec, exp_spec, exp_spec), out_specs=rows_spec, check_vma=False)
```

profile of v0, /device:TPU:0, one launch (start us, length us, event | category | flops | bytes accessed | tf_op | source)
XLA Modules:
  0.0 923.8 jit_solution(4739680350039196808)
XLA Ops:
  7.4 60.1 %all-gather.4.cloned.1.call-done = bf16[1024,4096]{1,0:T(8,128)(2,1)} async-done(((bf16[256,4096]{1,0:T(8,128)(2,1)}), bf16[1024,4096]{1,0:T(8,128)(2,1)}) %all-gather.4.cloned.1.call-update) | async-done | bytes 8388624 | tf_op jit(solution)/shard_map/all_gather | solution.py:19
  67.5 5.9 convolution_convert_fusion.1
  73.8 2.4 convolution_convert_fusion.2
  77.6 1.3 broadcast_compare_fusion.1
  79.0 14.7 %convolution_convert_fusion = bf16[1024,1024]{0,1:T(8,128)(2,1)} fusion(bf16[1024,4096]{1,0:T(8,128)(2,1)} %all-gather.4.cloned.1.call-done, bf16[4096,1024]{1,0:T(8,128)(2,1)} %param.13), kind=kOutput, calls=%fused_computation.36 | convolution fusion | flops 8590983168 | bytes 18874368 | tf_op jit(solution)/shard_map/dot_general | solution.py:22
  93.7 13.9 %all-gather.6.cloned.1.call-done = bf16[2048,512]{0,1:T(8,128)(2,1)} async-done(((bf16[1024,512]{0,1:T(8,128)(2,1)}), bf16[2048,512]{0,1:T(8,128)(2,1)}) %all-gather.6.cloned.1.call-update) | async-done | bytes 2097168 | tf_op jit(solution)/shard_map/all_gather | solution.py:28
  107.6 4.5 reshape.327
  112.1 5.9 fusion.58
  118.7 13.9 %fusion.6 = (f32[2,4,1024]{2,1,0:T(4,128)S(1)}, f32[2,1024,1024,4]{2,1,3,0:T(8,128)}) fusion(pred[1024,1024]{0,1:T(8,128)(4,1)S(1)} %get-tuple-element.16, bf16[1024,2,128,1]{0,2,3,1:T(8,128)(2,1)S(1)} %bitcast.133, bf16[1024,2,4,128]{0,3,2,1:T(8,128)(2,1)S(1)} %bitcast.127), kind=kOutput, calls=%fused_computation.14 | convolution fusion | flops 2172641280 | bytes 37257216 | tf_op jit(solution)/shard_map/nkgd,mkd->kgnm/dot_general | solution.py:45
  132.6 14.4 %fusion.7 = (f32[2,4,1024]{2,1,0:T(4,128)S(1)}, f32[2,1024,1024,4]{2,1,3,0:T(8,128)}) fusion(pred[1024,1024]{0,1:T(8,128)(4,1)S(1)} %get-tuple-element.17, bf16[1024,2,128,1]{0,2,3,1:T(8,128)(2,1)S(1)} %bitcast.132, bf16[1024,2,4,128]{0,3,2,1:T(8,128)(2,1)S(1)} %bitcast.128), kind=kOutput, calls=%fused_computation.15 | convolution fusion | flops 2172641280 | bytes 37257216 | tf_op jit(solution)/shard_map/nkgd,mkd->kgnm/dot_general | solution.py:45
  147.1 16.8 %fusion.12 = f32[2,4,1024,128]{2,3,1,0:T(8,128)} fusion(bf16[1024,2,128,1]{0,2,3,1:T(8,128)(2,1)S(1)} %bitcast.135, f32[2,1024,1024,4]{2,1,3,0:T(8,128)} %get-tuple-element.21, f32[2,4,1024]{2,1,0:T(4,128)S(1)} %get-tuple-element.15, pred[1024,1024]{0,1:T(8,128)(4,1)S(1)} %get-tuple-element.17), kind=kOutput, calls=%fused_computation.21 | convolution fusion | flops 2189426688 | bytes 39354368 | tf_op jit(solution)/shard_map/kgnm,mkd->kgnd/dot_general | solution.py:51
  163.9 24.8 %fusion.8 = (f32[2,4,1024]{2,1,0:T(4,128)S(1)}, f32[2,4,1024]{2,1,0:T(4,128)S(1)}) fusion(f32[2,1024,1024,4]{2,1,3,0:T(8,128)} %get-tuple-element.19, f32[2,4,1024]{2,1,0:T(4,128)S(1)} %get-tuple-element.14, pred[1024,1024]{0,1:T(8,128)(4,1)S(1)} %get-tuple-element.16, f32[2,4,1024]{2,1,0:T(4,128)S(1)} %get-tuple-element.15, ...), kind=kLoop, calls=%fused_computation.17 | loop fusion | flops 83869696 | bytes 69337088 | tf_op jit(solution)/shard_map/reduce_sum | solution.py:50
  188.7 18.0 %fusion.24 = bf16[1024,2,4,128]{0,3,2,1:T(8,128)(2,1)} fusion(f32[2,4,1024,128]{2,3,1,0:T(8,128)} %fusion.12, bf16[1024,2,128,1]{0,2,3,1:T(8,128)(2,1)S(1)} %bitcast.134, f32[2,1024,1024,4]{2,1,3,0:T(8,128)} %get-tuple-element.19, f32[2,4,1024]{2,1,0:T(4,128)S(1)} %get-tuple-element.14, pred[1024,1024]{0,1:T(8,128)(4,1)S(1)} %get-tuple-element.16, ...), kind=kOutput, calls=%fused_computation.29 | convolution fusion | flops 2194669568 | bytes 41549824 | tf_op jit(solution)/shard_map/kgnm,mkd->kgnd/dot_general | solution.py:51
  206.7 16.2 %fusion.59 = f32[1024,4096]{1,0:T(8,128)} fusion(bf16[1024,1024]{0,1:T(8,128)(2,1)} %bitcast.138, bf16[1024,4096]{1,0:T(8,128)(2,1)} %param.16), kind=kOutput, calls=%fused_computation.96 | convolution fusion | flops 8589934592 | bytes 27262976 | tf_op jit(solution)/shard_map/dot_general | solution.py:54
  224.1 1.1 reduce-window.6
  225.7 3.5 gather_fusion.2
  229.8 112.0 %reduce-scatter.2.cloned.1.call-done = f32[256,4096]{1,0:T(8,128)} async-done(((f32[1024,4096]{1,0:T(8,128)}), f32[256,4096]{1,0:T(8,128)}) %reduce-scatter.2.cloned.1.call-update) | async-done | bytes 4194320 | tf_op jit(solution)/shard_map/reduce_scatter | solution.py:55
  341.8 3.4 add_convert_fusion.1
  345.3 4.5 gather_fusion
  349.8 4.3 broadcast_in_dim.85
  354.1 132.3 %scatter_fusion = bf16[8,128,4096]{2,1,0:T(8,128)(2,1)} fusion(bf16[8,128,4096]{2,1,0:T(8,128)(2,1)} %broadcast_in_dim.85, s32[512]{0:T(512)S(1)} %bitcast.125, bf16[512,4096]{1,0:T(8,128)(2,1)} %gather_fusion), kind=kCustom, calls=%fused_computation.3 | custom fusion | bytes 12587008 | tf_op jit(solution)/shard_map/scatter | solution.py:75
  486.4 96.3 %all_to_all.10 = bf16[8,128,4096]{2,1,0:T(8,128)(2,1)S(1)} all-to-all(bf16[8,128,4096]{2,1,0:T(8,128)(2,1)} %scatter_fusion), channel_id=1, replica_groups=mesh['dp'=1,'cp'=2,'tp'=4] {'cp','tp'}, dimensions={0} | all-to-all | bytes 16777216 | tf_op jit(solution)/shard_map/all_to_all | solution.py:76
  582.7 3.3 copy-done.6
  586.0 61.3 %fusion.4 = f32[1024,6400]{1,0:T(8,128)} fusion(bf16[1024,4096]{1,0:T(8,128)(2,1)S(1)} %bitcast.130, bf16[1,4096,6400]{2,1,0:T(8,128)(2,1)} %param.17), kind=kOutput, calls=%fused_computation.8 | convolution fusion | flops 53687091200 | bytes 87031808 | tf_op jit(solution)/shard_map/dot_general | solution.py:11
  647.3 66.0 %multiply_convert_fusion = bf16[1024,6400]{1,0:T(8,128)(2,1)} fusion(f32[1024,6400]{1,0:T(8,128)} %fusion.4, bf16[1024,4096]{1,0:T(8,128)(2,1)} %bitcast.131, bf16[1,4096,6400]{2,1,0:T(8,128)(2,1)} %param.18), kind=kOutput, calls=%fused_computation.16 | convolution fusion | flops 53726412800 | bytes 100139008 | tf_op jit(solution)/shard_map/dot_general | solution.py:12
  713.3 63.0 %fusion.20 = bf16[1024,4096]{1,0:T(8,128)(2,1)} fusion(bf16[1024,6400]{1,0:T(8,128)(2,1)} %multiply_convert_fusion, bf16[1,6400,4096]{2,1,0:T(8,128)(2,1)} %param.19), kind=kOutput, calls=%fused_computation.26 | convolution fusion | flops 53691285504 | bytes 73924608 | tf_op jit(solution)/shard_map/dot_general | solution.py:14
  776.4 4.0 all-to-all-start.1
  780.5 93.8 %all-to-all-done.1 = bf16[8,128,4096]{2,1,0:T(8,128)(2,1)} async-done(((bf16[8,128,4096]{2,1,0:T(8,128)(2,1)}), bf16[8,128,4096]{2,1,0:T(8,128)(2,1)}, u32[]{:S(2)}, u32[]{:S(2)}) %all-to-all-start.1) | async-done | bytes 8388640 | tf_op jit(solution)/shard_map/all_to_all | solution.py:78
  874.4 17.3 %gather_fusion.1 = bf16[512,4096]{1,0:T(8,128)(2,1)} fusion(bf16[8,128,4096]{2,1,0:T(8,128)(2,1)} %all-to-all-done.1, s32[512]{0:T(512)S(1)} %bitcast.124), kind=kCustom, calls=%fused_computation.1 | custom fusion | bytes 8392704 | tf_op jit(solution)/shard_map/gather | solution.py:79
  891.7 9.8 %reshape.298 = f32[256,2,4096]{2,1,0:T(2,128)} reshape(bf16[512,4096]{1,0:T(8,128)(2,1)} %gather_fusion.1) | data formatting | bytes 12582912 | tf_op jit(solution)/shard_map/convert_element_type | solution.py:79
  901.5 13.6 %multiply_reduce_fusion = f32[256,4096]{1,0:T(8,128)S(1)} fusion(f32[256,2,4096]{2,1,0:T(2,128)} %reshape.298, f32[256,2]{1,0:T(8,128)S(1)} %copy.26), kind=kLoop, calls=%fused_computation.25 | loop fusion | flops 3145728 | bytes 12584960 | tf_op jit(solution)/shard_map/reduce_sum | solution.py:80
  915.0 2.0 add_convert_fusion
  (54 shorter events, 5.7 us)
Async XLA Ops:
  6.5 60.9 %copy-start = (bf16[4096,256]{1,0:T(8,128)(2,1)S(1)}, bf16[4096,256]{1,0:T(8,128)(2,1)}, u32[]{:S(2)}) copy-start(bf16[4096,256]{1,0:T(8,128)(2,1)} %param.15) | copy-start | bytes 6291460
  6.5 60.9 %all-gather.4.cloned.1.call-start = ((), (), s32[]{:S(2)}) async-start(), calls=%async_computation.3 | async-start | bytes 10485760 | tf_op jit(solution)/shard_map/all_gather | solution.py:19
  7.3 100.3 %all-gather.6.cloned.1.call-start = ((), (), s32[]{:S(2)}) async-start(), calls=%async_computation.5 | async-start | bytes 3145728 | tf_op jit(solution)/shard_map/all_gather | solution.py:28
  67.4 5.9 copy-start.9
  67.5 6.4 copy-start.10
  77.3 264.5 %reduce-scatter.2.cloned.1.call-start = ((), (), s32[]{:S(2)}) async-start(), calls=%async_computation.4 | async-start | bytes 20971520 | tf_op jit(solution)/shard_map/reduce_scatter | solution.py:55
  112.1 6.6 copy-start.5
  222.9 0.7 copy-start.7
  345.3 4.6 copy-start.2
  582.7 3.3 copy-start.6
  776.4 4.0 copy-start.8
  776.4 98.0 %copy-start.4 = (s32[512,1]{0,1:T(1,128)S(1)}, s32[512,1]{0,1:T(1,128)}, u32[]{:S(2)}) copy-start(s32[512,1]{0,1:T(1,128)} %get-tuple-element.8) | copy-start | bytes 6148
  776.4 98.0 %all-to-all-start.1 = ((bf16[8,128,4096]{2,1,0:T(8,128)(2,1)}), bf16[8,128,4096]{2,1,0:T(8,128)(2,1)}, u32[]{:S(2)}, u32[]{:S(2)}) async-start(bf16[8,128,4096]{2,1,0:T(8,128)(2,1)} %bitcast.129), calls=%async_computation.2 | async-start | bytes 16777216 | tf_op jit(solution)/shard_map/all_to_all | solution.py:78
  891.7 25.4 %copy-start.1 = (bf16[4096,256]{1,0:T(8,128)(2,1)S(1)}, bf16[4096,256]{1,0:T(8,128)(2,1)}, u32[]{:S(2)}) copy-start(bf16[4096,256]{1,0:T(8,128)(2,1)} %param.15) | copy-start | bytes 6291460
  901.5 13.6 %copy-start.3 = (bf16[256,4096]{1,0:T(8,128)(2,1)S(1)}, bf16[256,4096]{1,0:T(8,128)(2,1)}, u32[]{:S(2)}) copy-start(bf16[256,4096]{1,0:T(8,128)(2,1)} %copy-done.2) | copy-start | bytes 6291460
Sparse Core Ops, SparseCore 0:
  8.9 58.5 all-gather.3
  77.4 30.1 all-gather.5
  223.0 118.7 reduce-scatter.1
where the time goes:
time: 930 us; the launch traced here: 924 us
  matrix products  293 us (32%)
  waiting for transfers between devices  281 us (30%)
  local copies, waits for them, and re-layouts  188 us (20%)
  blocking collectives  96.3 us (10%)
  other arithmetic  48.1 us (5%)
  between operations  13.6 us (1%)
    scatter x1, local copies, waits for them, and re-layouts, local(): send = jnp.zeros((ne, cap, hd), jnp.bfloat16).at[ea, slot].set(h[tok])  132 us
    reduce_scatter x1, waiting for transfers between devices, attention_residual(): att = lax.psum_scatter(part, 'tp', scatter_dimension=0, tiled=True)  112 us
    all_to_all x1, blocking collectives, local(): recv = lax.all_to_all(send, ('cp', 'tp'), 0, 0, tiled=True)  96.3 us
    all_to_all x1, waiting for transfers between devices, local(): lax.all_to_all(z.reshape(ne, cap, hd), ('cp', 'tp'), 0, 0, tiled=True)  93.8 us
    dot_general x1, matrix products, expert_ffn(): uu = jnp.dot(rows, wu, preferred_element_type=jnp.float32)  66 us
    dot_general x1, matrix products, expert_ffn(): jnp.dot(act, wd, preferred_element_type=jnp.float32).astype(jnp.bfloat16)  63 us
    dot_general x1, matrix products, expert_ffn(): gg = jnp.dot(rows, wg, preferred_element_type=jnp.float32)  61.3 us
    all_gather x1, waiting for transfers between devices, attention_residual(): xs = lax.all_gather(x, 'tp', axis=0, tiled=True)  60.1 us
  transfers between devices with their start and end apart: 4, of which 4 were waited for; matrix products, arithmetic and copies ran while one was open for 2% of the time, Pallas kernels for 0%

commit v1 on v0

v1 whole, which is shorter than its diff:
```python
import functools

import jax
import jax.numpy as jnp
from jax import lax
from jax.experimental import pallas as pl
from jax.experimental.pallas import tpu as pltpu
from jax.sharding import PartitionSpec as P

HEAD_DIM = 128
NEG = -1e30
LOG2E = 1.4426950408889634
MESH = pl.DeviceIdType.MESH
BF = jnp.bfloat16
F32 = jnp.float32
VMEM_LIMIT = 60 * 1024 * 1024


def attn_body(rank_ref, q_ref, k_ref, v_ref, o_ref, *, seg, cp, bq, scale):
    rank = rank_ref[0]
    c = scale * LOG2E

    def block(s_id):
        src = jnp.where(s_id < cp, s_id, 2 * cp - 1 - s_id)
        off = jnp.where(s_id < cp, 0, seg)
        return src, pl.multiple_of(off, seg)

    def update(carry, s, vj):
        m, l, acc = carry
        mn = jnp.maximum(m, jnp.max(s, axis=-1, keepdims=True))
        w = jnp.exp2((s - mn) * c)
        a = jnp.exp2((m - mn) * c)
        l = l * a + jnp.sum(w, axis=-1, keepdims=True)
        acc = acc * a + jnp.dot(w.astype(BF), vj, preferred_element_type=F32)
        return mn, l, acc

    def score(q, kj):
        return lax.dot_general(q, kj, (((1,), (1,)), ((), ())), preferred_element_type=F32)

    for half in range(2):
        mine = rank if half == 0 else 2 * cp - 1 - rank
        for r in range(seg // bq):
            rows = pl.ds(half * seg + r * bq, bq)
            q = q_ref[rows, :]
            init = (jnp.full((bq, 1), NEG, F32), jnp.zeros((bq, 1), F32), jnp.zeros((bq, HEAD_DIM), F32))

            def full(j, carry):
                src, off = block(j)
                kj = k_ref[src, pl.ds(off, seg), :]
                vj = v_ref[src, pl.ds(off, seg), :]
                return update(carry, score(q, kj), vj)

            carry = lax.fori_loop(0, mine, full, init)
            src, off = block(mine)
            w = (r + 1) * bq
            kj = k_ref[src, pl.ds(off, w), :]
            vj = v_ref[src, pl.ds(off, w), :]
            s = score(q, kj)
            qi = r * bq + lax.broadcasted_iota(jnp.int32, (bq, w), 0)
            ki = lax.broadcasted_iota(jnp.int32, (bq, w), 1)
            s = jnp.where(ki <= qi, s, NEG)
            m, l, acc = update(carry, s, vj)
            o_ref[rows, :] = (acc / l).astype(BF)


def attention(q, kvs, rank, cp):
    n, wq = q.shape
    heads = wq // HEAD_DIM
    kvh = kvs.shape[2] // (2 * HEAD_DIM)
    g = heads // kvh
    seg = n // 2
    body = functools.partial(attn_body, seg=seg, cp=cp, bq=seg // 2, scale=HEAD_DIM ** -0.5)
    return pl.pallas_call(
        body,
        grid_spec=pltpu.PrefetchScalarGridSpec(
            num_scalar_prefetch=1,
            grid=(heads,),
            in_specs=[
                pl.BlockSpec((n, HEAD_DIM), lambda j, r: (0, j)),
                pl.BlockSpec((cp, n, HEAD_DIM), lambda j, r: (0, 0, j // g)),
                pl.BlockSpec((cp, n, HEAD_DIM), lambda j, r: (0, 0, kvh + j // g)),
            ],
            out_specs=pl.BlockSpec((n, HEAD_DIM), lambda j, r: (0, j)),
        ),
        out_shape=jax.ShapeDtypeStruct((n, wq), BF),
        compiler_params=pltpu.CompilerParams(vmem_limit_bytes=32 * 1024 * 1024),
        cost_estimate=pl.CostEstimate(flops=20_000_000_000, bytes_accessed=8_000_000, transcendentals=10_000_000),
        name='attn',
    )(rank.reshape(1), q, kvs, kvs)


def up_body(x_ref, g_ref, u_ref, a_ref):
    x = x_ref[...]
    gg = jnp.dot(x, g_ref[0], preferred_element_type=F32)
    uu = jnp.dot(x, u_ref[0], preferred_element_type=F32)
    a_ref[...] = (jax.nn.silu(gg) * uu).astype(BF)


def expert_up(rows, wg, wu, tile):
    r, hd = rows.shape
    ff = wg.shape[2]
    return pl.pallas_call(
        up_body,
        grid=(ff // tile,),
        in_specs=[
            pl.BlockSpec((r, hd), lambda j: (0, 0)),
            pl.BlockSpec((1, hd, tile), lambda j: (0, 0, j)),
            pl.BlockSpec((1, hd, tile), lambda j: (0, 0, j)),
        ],
        out_specs=pl.BlockSpec((r, tile), lambda j: (0, j)),
        out_shape=jax.ShapeDtypeStruct((r, ff), BF),
        compiler_params=pltpu.CompilerParams(vmem_limit_bytes=VMEM_LIMIT),
        cost_estimate=pl.CostEstimate(flops=4 * r * hd * ff, bytes_accessed=4 * hd * ff, transcendentals=r * ff),
        name='expert_up',
    )(rows, wg, wu)


def down_body(a_ref, w_ref, h_ref, tgt_ref, gate_ref, y_ref, zs, zb, send_sem, recv_sem, own_sem, *, cp, tp, cap, nt, lag):
    step = pl.program_id(0)
    ne = cp * tp
    c = lax.axis_index('cp')
    t = lax.axis_index('tp')
    me = c * tp + t

    def peer(d):
        return {'cp': c ^ (d // tp), 'tp': t ^ (d % tp)}, (c ^ (d // tp)) * tp + (t ^ (d % tp))

    def rows(e):
        return pl.ds(pl.multiple_of(e * cap, cap), cap)

    def remote(n, d):
        where, e = peer(d)
        return pltpu.make_async_remote_copy(
            src_ref=zs.at[n, rows(e)], dst_ref=zb.at[n, rows(me)], send_sem=send_sem.at[n, d],
            recv_sem=recv_sem.at[n, d], device_id=where, device_id_type=MESH)

    def own(n):
        return pltpu.make_async_copy(zs.at[n, rows(me)], zb.at[n, rows(me)], own_sem.at[n])

    @pl.when(step == 0)
    def _():
        barrier = pltpu.get_barrier_semaphore()
        for d in range(1, ne):
            pl.semaphore_signal(barrier, inc=1, device_id=peer(d)[0], device_id_type=MESH)
        pl.semaphore_wait(barrier, ne - 1)

    @pl.when((step >= 1) & (step <= nt))
    def _():
        for d in range(1, ne):
            remote(step - 1, d).start()
        own(step - 1).start()

    @pl.when(step < nt)
    def _():
        zs[step] = jnp.dot(a_ref[...], w_ref[0], preferred_element_type=F32).astype(BF)

    @pl.when(step >= lag)
    def _():
        n = step - lag
        own(n).wait()
        for d in range(1, ne):
            remote(n, d).wait_recv()
        slots = lax.broadcasted_iota(jnp.int32, (tgt_ref.shape[0], ne * cap), 1)
        z = zb[n]
        acc = h_ref[...].astype(F32)
        zsum = None
        for k in range(tgt_ref.shape[1]):
            pick = (slots == tgt_ref[:, k:k + 1]).astype(BF)
            zk = gate_ref[:, k:k + 1] * jnp.dot(pick, z, preferred_element_type=F32)
            zsum = zk if zsum is None else zsum + zk
        y_ref[...] = (acc + zsum).astype(BF)
        for d in range(1, ne):
            remote(n, d).wait_send()


def expert_down(act, wd, h, tgt, gates, cp, tp, cap, tile, lag):
    r, ff = act.shape
    t, hd = h.shape
    kk = tgt.shape[1]
    ne = cp * tp
    nt = hd // tile
    body = functools.partial(down_body, cp=cp, tp=tp, cap=cap, nt=nt, lag=lag)
    late = lambda j: (0, jnp.maximum(j - lag, 0))
    return pl.pallas_call(
        body,
        grid=(nt + lag,),
        in_specs=[
            pl.BlockSpec((r, ff), lambda j: (0, 0)),
            pl.BlockSpec((1, ff, tile), lambda j: (0, 0, jnp.minimum(j, nt - 1))),
            pl.BlockSpec((t, tile), late),
            pl.BlockSpec((t, kk), lambda j: (0, 0)),
            pl.BlockSpec((t, kk), lambda j: (0, 0)),
        ],
        out_specs=pl.BlockSpec((t, tile), late),
        out_shape=jax.ShapeDtypeStruct((t, hd), BF),
        scratch_shapes=[
            pltpu.VMEM((nt, r, tile), BF),
            pltpu.VMEM((nt, r, tile), BF),
            pltpu.SemaphoreType.DMA((nt, ne)),
            pltpu.SemaphoreType.DMA((nt, ne)),
            pltpu.SemaphoreType.DMA((nt,)),
        ],
        compiler_params=pltpu.CompilerParams(vmem_limit_bytes=VMEM_LIMIT, collective_id=cap, has_side_effects=True),
        cost_estimate=pl.CostEstimate(flops=2 * r * hd * ff, bytes_accessed=2 * hd * ff, transcendentals=0),
        name='expert_down',
    )(act, wd, h, tgt, gates)


def solution(mesh):
    cp = mesh.shape['cp']
    tp = mesh.shape['tp']
    ne = cp * tp
    rows_spec = P(('dp', 'cp', 'tp'), None)
    exp_spec = P(('cp', 'tp'), None, None)

    def local(x, idx, gates, wq, wk, wv, wo, w1g, w1u, w2):
        t, hd = x.shape
        kk = idx.shape[1]
        rank = lax.axis_index('cp')

        ea = idx.reshape(-1)
        onehot = (ea[:, None] == jnp.arange(ne)[None, :]).astype(jnp.int32)
        cum = jnp.cumsum(onehot, axis=0)
        slot = (jnp.sum(cum * onehot, axis=1) - 1).reshape(t, kk)
        fullest = lax.pmax(jnp.max(cum[-1]), ('cp', 'tp'))

        xs = lax.all_gather(x, 'tp', axis=0, tiled=True)
        k = jnp.dot(xs, wk, preferred_element_type=F32).astype(BF)
        v = jnp.dot(xs, wv, preferred_element_type=F32).astype(BF)
        kvs = lax.all_gather(jnp.concatenate([k, v], axis=1), 'cp', axis=0)
        q = jnp.dot(xs, wq, preferred_element_type=F32).astype(BF)
        o = attention(q, kvs, rank, cp)
        part = jnp.dot(o, wo, preferred_element_type=F32)
        att = lax.psum_scatter(part, 'tp', scatter_dimension=0, tiled=True)
        h = (x.astype(F32) + att).astype(BF)

        def moe(cap):
            def run(h, idx, slot, gates, w1g, w1u, w2):
                tgt = idx * cap + slot
                place = jnp.arange(ne * cap)[:, None]
                pick = ((place == tgt[None, :, 0]) | (place == tgt[None, :, 1])).astype(BF)
                send = jnp.dot(pick, h, preferred_element_type=F32).astype(BF).reshape(ne, cap, hd)
                recv = lax.all_to_all(send, ('cp', 'tp'), 0, 0, tiled=True)
                act = expert_up(recv.reshape(ne * cap, hd), w1g, w1u, 256)
                return expert_down(act, w2, h, tgt, gates, cp, tp, cap, 256, 4)
            return run

        caps = (2 * t // ne, 3 * t // ne, 4 * t // ne)
        tier = (fullest > caps[0]).astype(jnp.int32) + (fullest > caps[1]).astype(jnp.int32)
        return lax.switch(tier, [moe(cap) for cap in caps], h, idx, slot, gates, w1g, w1u, w2)

    return jax.shard_map(local, mesh=mesh, in_specs=(rows_spec, rows_spec, rows_spec, P(None, 'tp'), P(None, 'tp'), P(None, 'tp'), P('tp', None), exp_spec, exp_spec, exp_spec), out_specs=rows_spec, check_vma=False)
```

time: 930 us -> 634 us (0.68)
  Pallas kernels: 0 us -> 265 us
  matrix products: 293 us -> 42.9 us
  local copies, waits for them, and re-layouts: 188 us -> 10.9 us
  blocking collectives: 96.3 us -> 22.9 us
  other arithmetic: 48.1 us -> 6.48 us
  waiting for transfers between devices: 281 us -> 250 us
  starting transfers between devices: 4.36 us -> 15.6 us
    pallas_call x0 -> x3, Pallas kernels: none -> 265 us  [the longest x1 118 us: expert_up(): pl.pallas_call(up_body, grid=(ff // tile,), in_specs=[pl.BlockSpec((r, hd...]
    dot_general x11 -> x5, matrix products: 293 us -> 42.9 us  [the longest x1 14.6 us: local(): q = jnp.dot(xs, wq, preferred_element_type=F32).astype(BF)]
    scatter x1 -> x0, local copies, waits for them, and re-layouts: 132 us -> none  [local(): send = jnp.zeros((ne, cap, hd), jnp.bfloat16).at[ea, slot].set(h[tok])]
    all_to_all x1 -> x0, blocking collectives: 96.3 us -> none  [local(): recv = lax.all_to_all(send, ('cp', 'tp'), 0, 0, tiled=True)]
    reduce_sum x2 -> x1, other arithmetic: 38.4 us -> 0.02 us  [local(): slot = (jnp.sum(cum * onehot, axis=1) - 1).reshape(t, kk)]
    gather x3 -> x0, local copies, waits for them, and re-layouts: 25.3 us -> none  [the longest x1 17.3 us: local(): zt = back[ea, slot].astype(jnp.float32).reshape(t, kk, hd)]
    pmax x0 -> x1, blocking collectives: none -> 22.9 us  [local(): fullest = lax.pmax(jnp.max(cum[-1]), ('cp', 'tp'))]
    reduce_scatter x1, waiting for transfers between devices: 112 us -> 92 us  [local(): att = lax.psum_scatter(part, 'tp', scatter_dimension=0, tiled=True)]
  transfers between devices with their start and end apart: 4 -> 4, of which waited for: 4 -> 4; matrix products, arithmetic and copies ran while one was open for 2% -> 3% of each run, Pallas kernels for 0% -> 0%
where the time goes in v1:
time: 634 us; the launch traced here: 629 us
  Pallas kernels  265 us (42%)
  waiting for transfers between devices  250 us (39%)
  matrix products  42.9 us (7%)
  blocking collectives  22.9 us (4%)
  starting transfers between devices  15.6 us (2%)
  between operations  15 us (2%)
  local copies, waits for them, and re-layouts  10.9 us (2%)
  other arithmetic  6.48 us (1%)
    pallas_call x1, Pallas kernels, expert_up(): pl.pallas_call(up_body, grid=(ff // tile,), in_specs=[pl.BlockSpec((r, hd...  118 us
    pallas_call x1, Pallas kernels, expert_down(): pl.pallas_call(body, grid=(nt + lag,), in_specs=[pl.BlockSpec((r, ff), la...  106 us
    all_to_all x1, waiting for transfers between devices, run(): recv = lax.all_to_all(send, ('cp', 'tp'), 0, 0, tiled=True)  93.2 us
    reduce_scatter x1, waiting for transfers between devices, local(): att = lax.psum_scatter(part, 'tp', scatter_dimension=0, tiled=True)  92 us
    all_gather x1, waiting for transfers between devices, local(): xs = lax.all_gather(x, 'tp', axis=0, tiled=True)  60.1 us
    pallas_call x1, Pallas kernels, attention(): pl.pallas_call(body, grid_spec=pltpu.PrefetchScalarGridSpec(num_scalar_pr...  40 us
    pmax x1, blocking collectives, local(): fullest = lax.pmax(jnp.max(cum[-1]), ('cp', 'tp'))  22.9 us
    dot_general x1, matrix products, local(): q = jnp.dot(xs, wq, preferred_element_type=F32).astype(BF)  14.6 us
  transfers between devices with their start and end apart: 4, of which 4 were waited for; matrix products, arithmetic and copies ran while one was open for 3% of the time, Pallas kernels for 0%

profile of v1, /device:TPU:0, one launch (start us, length us, event | category | flops | bytes accessed | tf_op | source)
XLA Modules:
  0.0 629.2 jit_solution(17213062430829482614)
XLA Ops:
  6.5 0.7 all-gather.4.cloned.1.call-update
  7.3 60.1 %all-gather.4.cloned.1.call-done = bf16[1024,4096]{1,0:T(8,128)(2,1)} async-done(((bf16[256,4096]{1,0:T(8,128)(2,1)}), bf16[1024,4096]{1,0:T(8,128)(2,1)}) %all-gather.4.cloned.1.call-update) | async-done | bytes 8388624 | tf_op jit(solution)/shard_map/all_gather | solution.py:227
  67.5 5.9 convolution_convert_fusion.4
  73.4 0.4 copy-done.9
  73.8 2.4 convolution_convert_fusion.5
  76.2 1.0 pad_maximum_fusion
  77.3 11.6 %reduce-scatter.2.cloned.1.call-start = ((), (), s32[]{:S(2)}) async-start(), calls=%async_computation.5 | async-start | bytes 20971520 | tf_op jit(solution)/shard_map/reduce_scatter | solution.py:234
  88.9 14.6 %convolution_convert_fusion.3.q_ref = bf16[1024,1024]{1,0:T(8,128)(2,1)} fusion(bf16[1024,4096]{1,0:T(8,128)(2,1)} %all-gather.4.cloned.1.call-done, bf16[4096,1024]{1,0:T(8,128)(2,1)} %param.16), kind=kOutput, calls=%fused_computation.34 | convolution fusion | flops 8590983168 | bytes 18874368 | tf_op jit(solution)/shard_map/dot_general | solution.py:231
  103.6 4.0 all-gather.6.cloned.1.call-done
  107.6 2.9 copy.34
  110.5 1.6 copy-done.2
  112.1 40.0 %attn.1 = bf16[1024,1024]{1,0:T(8,128)(2,1)S(1)} custom-call(s32[1]{0:T(128)} %bitcast.8.rank_ref, bf16[1024,1024]{1,0:T(8,128)(2,1)S(1)} %copy-done.2, bf16[2,1024,512]{2,1,0:T(8,128)(2,1)S(1)} %bitcast.23, bf16[2,1024,512]{2,1,0:T(8,128)(2,1)S(1)} %bitcast.24), custom_call_target="tpu_custom_call" | custom-call | flops 20000000000 | bytes 8000000 | tf_op jit(solution)/shard_map/attn/pallas_call | solution.py:73
  152.0 14.4 %fusion.13 = f32[1024,4096]{1,0:T(8,128)} fusion(bf16[1024,1024]{1,0:T(8,128)(2,1)S(1)} %attn.1, bf16[1024,4096]{1,0:T(8,128)(2,1)} %param.19), kind=kOutput, calls=%fused_computation.43 | convolution fusion | flops 8589934592 | bytes 27262976 | tf_op jit(solution)/shard_map/dot_general | solution.py:233
  166.5 0.7 copy-done.6
  167.3 0.1 eq.115
  167.4 1.1 reduce-window.6
  168.6 0.2 slice_reduce_fusion.6
  168.9 0.7 slice_reduce_fusion.7
  169.6 22.9 %pmax.7 = s32[]{:T(128)} all-reduce(s32[]{:T(128)} %slice_reduce_fusion.7), channel_id=1, replica_groups=mesh['dp'=1,'cp'=2,'tp'=4] {'cp','tp'}, use_global_device_ids=true, to_apply=%region_3.4 | all-reduce | flops 1 | bytes 8 | tf_op jit(solution)/shard_map/pmax | solution.py:225
  193.9 92.0 %reduce-scatter.2.cloned.1.call-done = f32[256,4096]{1,0:T(8,128)} async-done(((f32[1024,4096]{1,0:T(8,128)}), f32[256,4096]{1,0:T(8,128)}) %reduce-scatter.2.cloned.1.call-update) | async-done | bytes 4194320 | tf_op jit(solution)/shard_map/reduce_scatter | solution.py:234
  285.9 3.4 add_convert_fusion
  289.4 329.5 %conditional.1 = (bf16[256,4096]{1,0:T(8,128)(2,1)}) conditional(s32[]{:T(128)} %clamp.3, (s32[256,2]{0,1:T(2,128)S(1)}, s32[256,2]{0,1:T(2,128)S(1)}, bf16[256,4096]{1,0:T(8,128)(2,1)S(1)}, bf16[1,4096,6400]{2,1,0:T(8,128)(2,1)}, bf16[1,4096,6400]{2,1,0:T(8,128)(2,1)}, /*index=5*/bf16[1,6400,4096]{2,1,0:T(8,128)(2,1)}, ...), branch_computations={%region_6.7_spmd, %region_7.8_spmd, %region_8.9_spmd} | conditional | flops 163213754368 | bytes 193019968 | solution.py:250
  289.7 0.1 eq.131
  289.9 0.1 sub.10
  290.2 0.2 slice_reduce_fusion.5
  290.4 5.6 convolution_convert_fusion.2
  296.0 4.0 all-to-all-start.2
  300.0 0.8 copy.43.gate_ref
  300.8 93.2 %all-to-all-done.2 = bf16[8,128,4096]{2,1,0:T(8,128)(2,1)} async-done(((bf16[8,128,4096]{2,1,0:T(8,128)(2,1)}), bf16[8,128,4096]{2,1,0:T(8,128)(2,1)}, u32[]{:S(2)}, u32[]{:S(2)}) %all-to-all-start.2) | async-done | bytes 8388640 | tf_op jit(solution)/shard_map/cond/branch_2_fun/all_to_all | solution.py:243
  394.0 118.4 %expert_up.5.a_ref = bf16[1024,6400]{1,0:T(8,128)(2,1)} custom-call(bf16[1024,4096]{1,0:T(8,128)(2,1)} %bitcast.5.x_ref, bf16[1,4096,6400]{2,1,0:T(8,128)(2,1)} %get-tuple-element.96.g_ref, bf16[1,4096,6400]{2,1,0:T(8,128)(2,1)} %get-tuple-element.99.u_ref), custom_call_target="tpu_custom_call" | custom-call | flops 107374182400 | bytes 104857600 | tf_op jit(solution)/shard_map/cond/branch_2_fun/expert_up/pallas_call | solution.py:102
  512.3 106.3 %expert_down.5 = bf16[256,4096]{1,0:T(8,128)(2,1)} custom-call(bf16[1024,6400]{1,0:T(8,128)(2,1)} %expert_up.5.a_ref, bf16[1,6400,4096]{2,1,0:T(8,128)(2,1)} %get-tuple-element.102.w_ref, bf16[256,4096]{1,0:T(8,128)(2,1)S(1)} %get-tuple-element.67.h_ref, s32[256,2]{1,0:T(8,128)} %copy-done.5, f32[256,2]{1,0:T(8,128)} %copy.43.gate_ref), custom_call_target="tpu_custom_call" | custom-call | flops 53687091200 | bytes 52428800 | tf_op jit(solution)/shard_map/cond/branch_2_fun/expert_down/pallas_call | solution.py:184
  618.9 3.3 copy.48
  (28 shorter events, 0.7 us)
Async XLA Ops:
  6.5 60.9 %copy-start = (bf16[4096,256]{1,0:T(8,128)(2,1)S(1)}, bf16[4096,256]{1,0:T(8,128)(2,1)}, u32[]{:S(2)}) copy-start(bf16[4096,256]{1,0:T(8,128)(2,1)} %param.18) | copy-start | bytes 6291460
  6.5 60.9 %all-gather.4.cloned.1.call-start = ((), (), s32[]{:S(2)}) async-start(), calls=%async_computation.4 | async-start | bytes 10485760 | tf_op jit(solution)/shard_map/all_gather | solution.py:227
  7.3 100.3 %all-gather.6.cloned.1.call-start = ((), (), s32[]{:S(2)}) async-start(), calls=%async_computation.6 | async-start | bytes 3145728 | tf_op jit(solution)/shard_map/all_gather | solution.py:230
  67.4 5.9 copy-start.8
  67.5 6.4 %copy-start.9 = (bf16[4096,256]{1,0:T(8,128)(2,1)S(1)}, bf16[4096,256]{1,0:T(8,128)(2,1)}, u32[]{:S(2)}) copy-start(bf16[4096,256]{1,0:T(8,128)(2,1)} %param.17) | copy-start | bytes 6291460
  77.3 208.6 %reduce-scatter.2.cloned.1.call-start = ((), (), s32[]{:S(2)}) async-start(), calls=%async_computation.5 | async-start | bytes 20971520 | tf_op jit(solution)/shard_map/reduce_scatter | solution.py:234
  110.5 1.6 copy-start.2
  166.5 0.7 copy-start.6
  193.9 95.5 %copy-start.7 = (f32[256,2]{0,1:T(2,128)S(1)}, f32[256,2]{0,1:T(2,128)}, u32[]{:S(2)}) copy-start(f32[256,2]{0,1:T(2,128)} %param.15) | copy-start | bytes 6148
  290.2 5.8 copy-start.5
  296.0 97.9 %all-to-all-start.2 = ((bf16[8,128,4096]{2,1,0:T(8,128)(2,1)}), bf16[8,128,4096]{2,1,0:T(8,128)(2,1)}, u32[]{:S(2)}, u32[]{:S(2)}) async-start(bf16[8,128,4096]{2,1,0:T(8,128)(2,1)} %bitcast.25), calls=%async_computation.2 | async-start | bytes 16777216 | tf_op jit(solution)/shard_map/cond/branch_2_fun/all_to_all | solution.py:243
  618.9 3.3 copy-start.1
Sparse Core Ops, SparseCore 0:
  8.9 58.5 all-gather.3
  77.4 30.1 all-gather.5
  166.6 119.2 reduce-scatter.1

commit v2 on v1

v2 whole, which is shorter than its diff:
```python
import functools

import jax
import jax.numpy as jnp
from jax import lax
from jax.experimental import pallas as pl
from jax.experimental.pallas import tpu as pltpu
from jax.sharding import PartitionSpec as P

HEAD_DIM = 128
NEG = -1e30
LOG2E = 1.4426950408889634
MESH = pl.DeviceIdType.MESH
BF = jnp.bfloat16
F32 = jnp.float32
VMEM_LIMIT = 60 * 1024 * 1024


def qkv_body(x_ref, cnt_ref, wq_hbm, wk_hbm, wv_hbm, q_ref, kv_ref, top_ref, wq, wk, wv, near, far, cnts,
             load_sem, psend, precv, xsend, xrecv, fsend, frecv, ksend, krecv, csend, crecv, *, cp, tp, ch):
    c = lax.axis_index('cp')
    t = lax.axis_index('tp')
    rows, hd = x_ref.shape
    part = rows // ch
    wide = q_ref.shape[1]
    kw = wk.shape[1]
    partner, across, other = {'tp': t ^ 1}, {'tp': t ^ 2}, {'cp': 1 - c}

    loads = [pltpu.make_async_copy(s, d, load_sem.at[i]) for i, (s, d) in enumerate(((wk_hbm, wk), (wv_hbm, wv), (wq_hbm, wq)))]
    for ld in loads:
        ld.start()

    def peer(d):
        return {'cp': c ^ (d // tp), 'tp': t ^ (d % tp)}

    barrier = pltpu.get_barrier_semaphore()
    for d in range(1, cp * tp):
        pl.semaphore_signal(barrier, inc=1, device_id=peer(d), device_id_type=MESH)
    pl.semaphore_wait(barrier, cp * tp - 1)

    def copy(src, dst, ss, rs, where):
        return pltpu.make_async_remote_copy(src_ref=src, dst_ref=dst, send_sem=ss, recv_sem=rs, device_id=where, device_id_type=MESH)

    out = [copy(x_ref.at[pl.ds(i * part, part)], far.at[i, 0], xsend.at[i], xrecv.at[i], across) for i in range(ch)]
    fwd = [copy(far.at[i, 0], far.at[i, 1], fsend.at[i], frecv.at[i], partner) for i in range(ch)]
    side = copy(x_ref, near, psend, precv, partner)
    count = [copy(cnt_ref, cnts.at[d], csend.at[d], crecv.at[d], peer(d)) for d in range(1, cp * tp)]
    for cpy in out:
        cpy.start()
    side.start()
    for cpy in count:
        cpy.start()

    def keys(n, first, size):
        sl = (c, pl.ds(pl.multiple_of(first, part), size))
        return copy(kv_ref.at[sl], kv_ref.at[sl], ksend.at[n], krecv.at[n], other)

    def project(xv, pieces, sends):
        def put(ref, val, col, width):
            for a, size, first in pieces:
                ref[pl.ds(pl.multiple_of(first, part), size), pl.ds(col, width)] = val[a:a + size].astype(BF)

        mine = kv_ref.at[c]
        put(mine, jnp.dot(xv, wk[...], preferred_element_type=F32), 0, kw)
        put(mine, jnp.dot(xv, wv[...], preferred_element_type=F32), kw, kw)

        def qtile(j):
            col = pl.multiple_of(j * kw, kw)
            put(q_ref, jnp.dot(xv, wq[:, pl.ds(col, kw)], preferred_element_type=F32), col, kw)

        qtile(0)
        for s in sends:
            s.start()

        @pl.loop(1, wide // kw)
        def _(j):
            qtile(j)

    for ld in loads:
        ld.wait()
    kcopies = []
    k0 = keys(0, t * rows, rows)
    kcopies.append(k0)
    project(x_ref[...], ((0, rows, t * rows),), (k0,))
    side.wait_recv()
    k1 = keys(1, (t ^ 1) * rows, rows)
    kcopies.append(k1)
    project(near[...], ((0, rows, (t ^ 1) * rows),), (k1,))
    for i in range(ch):
        out[i].wait_recv()
        fwd[i].start()
        fwd[i].wait_recv()
        r2 = (t ^ 2) * rows + i * part
        r3 = (t ^ 3) * rows + i * part
        ks = (keys(2 + 2 * i, r2, part), keys(3 + 2 * i, r3, part))
        kcopies.extend(ks)
        project(far[i].reshape(2 * part, hd), ((0, part, r2), (part, part, r3)), ks)
    top = cnt_ref[...]
    for d in range(1, cp * tp):
        count[d - 1].wait()
        top = jnp.maximum(top, cnts[d])
    top_ref[...] = top

    def keys_in(n, first, size):
        sl = (1 - c, pl.ds(pl.multiple_of(first, part), size))
        return copy(kv_ref.at[sl], kv_ref.at[sl], ksend.at[n], krecv.at[n], other)

    keys_in(0, t * rows, rows).wait_recv()
    keys_in(1, (t ^ 1) * rows, rows).wait_recv()
    for i in range(ch):
        keys_in(2 + 2 * i, (t ^ 2) * rows + i * part, part).wait_recv()
        keys_in(3 + 2 * i, (t ^ 3) * rows + i * part, part).wait_recv()
    for kc in kcopies:
        kc.wait_send()
    side.wait_send()
    for i in range(ch):
        out[i].wait_send()
        fwd[i].wait_send()


def project_qkv(x, cnt, wq, wk, wv, cp, tp):
    t, hd = x.shape
    n = t * tp
    wide, kw = wq.shape[1], wk.shape[1]
    ch = 4
    vm = pl.BlockSpec(memory_space=pltpu.VMEM)
    hbm = pl.BlockSpec(memory_space=pl.ANY)
    dma = pltpu.SemaphoreType.DMA
    return pl.pallas_call(
        functools.partial(qkv_body, cp=cp, tp=tp, ch=ch),
        in_specs=[vm, vm, hbm, hbm, hbm],
        out_specs=[vm, vm, vm],
        out_shape=[jax.ShapeDtypeStruct((n, wide), BF), jax.ShapeDtypeStruct((cp, n, 2 * kw), BF), jax.ShapeDtypeStruct(cnt.shape, cnt.dtype)],
        scratch_shapes=[
            pltpu.VMEM(wq.shape, BF), pltpu.VMEM(wk.shape, BF), pltpu.VMEM(wv.shape, BF),
            pltpu.VMEM((t, hd), BF), pltpu.VMEM((ch, 2, t // ch, hd), BF), pltpu.VMEM((cp * tp,) + cnt.shape, cnt.dtype),
            dma((3,)), dma, dma, dma((ch,)), dma((ch,)), dma((ch,)), dma((ch,)),
            dma((2 + 2 * ch,)), dma((2 + 2 * ch,)), dma((cp * tp,)), dma((cp * tp,)),
        ],
        compiler_params=pltpu.CompilerParams(vmem_limit_bytes=VMEM_LIMIT, collective_id=0, has_side_effects=True),
        cost_estimate=pl.CostEstimate(flops=2 * n * hd * (wide + 2 * kw), bytes_accessed=20_000_000, transcendentals=0),
        name='project_qkv',
    )(x, cnt, wq, wk, wv)


def attn_out_body(q_ref, kv_ref, x_ref, wo_hbm, h_ref, wo, ob, pt, rc, sm, rx,
                  load_sem, dsend, drecv, xsend, xrecv, *, cp, tp, nb, tile, scale):
    c = lax.axis_index('cp')
    t = lax.axis_index('tp')
    core, side = t % 2, t // 2
    rows, hd = x_ref.shape
    seg = 2 * rows
    sub = rows // nb
    nt = hd // tile
    heads = q_ref.shape[1] // HEAD_DIM
    kvh = kv_ref.shape[2] // (2 * HEAD_DIM)
    g = heads // kvh
    cc = scale * LOG2E

    load = pltpu.make_async_copy(wo_hbm, wo, load_sem)
    load.start()
    partner, across = {'tp': t ^ 1}, {'tp': t ^ 2}
    barrier = pltpu.get_barrier_semaphore()
    for where in (partner, across):
        pl.semaphore_signal(barrier, inc=1, device_id=where, device_id_type=MESH)
    pl.semaphore_wait(barrier, 2)

    def pass_half(i, n):
        return pltpu.make_async_remote_copy(
            src_ref=pt.at[i % 2, n, 1 - core], dst_ref=rc.at[i, n], send_sem=dsend.at[i % 2, n], recv_sem=drecv.at[i, n],
            device_id=partner, device_id_type=MESH)

    def pass_sum(i):
        return pltpu.make_async_remote_copy(
            src_ref=sm.at[i], dst_ref=rx.at[i], send_sem=xsend.at[i], recv_sem=xrecv.at[i],
            device_id=across, device_id_type=MESH)

    def score(q, kj):
        return lax.dot_general(q, kj, (((1,), (1,)), ((), ())), preferred_element_type=F32)

    def update(state, s, vj):
        m, l, acc = state
        mn = jnp.maximum(m, jnp.max(s, axis=-1, keepdims=True))
        w = jnp.exp2((s - mn) * cc)
        a = jnp.exp2((m - mn) * cc)
        l = l * a + jnp.sum(w, axis=-1, keepdims=True)
        acc = acc * a + jnp.dot(w.astype(BF), vj, preferred_element_type=F32)
        return mn, l, acc

    def block(s_id, width):
        src = jnp.where(s_id < cp, s_id, 2 * cp - 1 - s_id)
        return src, pl.ds(pl.multiple_of(jnp.where(s_id < cp, 0, seg), seg), width)

    def attend(i, half):
        place = jnp.where(i < nb, 1 - side, side)
        s_id = jnp.where(place == 0, c, 2 * cp - 1 - c)
        first = half * rows + (i % nb) * sub
        qrows = pl.ds(pl.multiple_of(place * seg + first, sub), sub)
        m4 = g * sub
        qs = [jnp.concatenate([q_ref[qrows, (a * g + b) * HEAD_DIM:(a * g + b + 1) * HEAD_DIM] for b in range(g)], axis=0)
              for a in range(kvh)]
        state = tuple((jnp.full((m4, 1), NEG, F32), jnp.zeros((m4, 1), F32), jnp.zeros((m4, HEAD_DIM), F32)) for _ in range(kvh))

        def kv(a, s, width):
            src, sl = block(s, width)
            return (kv_ref[src, sl, a * HEAD_DIM:(a + 1) * HEAD_DIM],
                    kv_ref[src, sl, (kvh + a) * HEAD_DIM:(kvh + a + 1) * HEAD_DIM])

        def full(j, state):
            pairs = [kv(a, j, seg) for a in range(kvh)]
            ss = [score(qs[a], pairs[a][0]) for a in range(kvh)]
            return tuple(update(state[a], ss[a], pairs[a][1]) for a in range(kvh))

        state = lax.fori_loop(0, s_id, full, state)
        width = (half + 1) * rows
        qi = first + lax.broadcasted_iota(jnp.int32, (m4, width), 0) % sub
        ki = lax.broadcasted_iota(jnp.int32, (m4, width), 1)
        keep = ki <= qi
        for a in range(kvh):
            kj, vj = kv(a, s_id, width)
            m, l, acc = update(state[a], jnp.where(keep, score(qs[a], kj), NEG), vj)
            r = (acc / l).astype(BF)
            for b in range(g):
                ob[pl.ds(half * sub, sub), (a * g + b) * HEAD_DIM:(a * g + b + 1) * HEAD_DIM] = r[b * sub:(b + 1) * sub]

    def cols(n):
        return pl.ds(pl.multiple_of(n * tile, tile), tile)

    @pl.loop(0, 2 * nb)
    def _(i):
        for half in range(2):
            attend(i, half)

        @pl.when(i == 0)
        def _():
            load.wait()

        @pl.when(i >= 2)
        def _():
            @pl.loop(0, nt)
            def _(n):
                pass_half(i - 2, n).wait_send()

        @pl.loop(0, nt)
        def _(n):
            p = jnp.dot(ob[...], wo[:, cols(n)], preferred_element_type=F32)
            pt[i % 2, n, 0] = p[:sub]
            pt[i % 2, n, 1] = p[sub:]

            @pl.when(n > 0)
            def _():
                pass_half(i, n - 1).start()

        pass_half(i, nt - 1).start()

        @pl.loop(0, nt)
        def _(n):
            pass_half(i, n).wait_recv()
            sm[i, n] = pt[i % 2, n, core] + rc[i, n]

        @pl.when(i < nb)
        def _():
            pass_sum(i).start()

    @pl.loop(0, nb)
    def _(j):
        pass_sum(j).wait_recv()
        own = pl.ds(pl.multiple_of(j * sub, sub), sub)

        @pl.loop(0, nt)
        def _(n):
            h_ref[own, cols(n)] = (x_ref[own, cols(n)].astype(F32) + (sm[nb + j, n] + rx[j, n])).astype(BF)

    @pl.loop(0, nt)
    def _(n):
        pass_half(2 * nb - 2, n).wait_send()
        pass_half(2 * nb - 1, n).wait_send()

    @pl.loop(0, nb)
    def _(j):
        pass_sum(j).wait_send()


def attention_out(q, kvs, x, wo, cp, tp):
    t, hd = x.shape
    nb, tile = 4, 512
    sub, nt = t // nb, hd // tile
    vm = pl.BlockSpec(memory_space=pltpu.VMEM)
    dma = pltpu.SemaphoreType.DMA
    return pl.pallas_call(
        functools.partial(attn_out_body, cp=cp, tp=tp, nb=nb, tile=tile, scale=HEAD_DIM ** -0.5),
        in_specs=[vm, vm, vm, pl.BlockSpec(memory_space=pl.ANY)],
        out_specs=vm,
        out_shape=jax.ShapeDtypeStruct((t, hd), BF),
        scratch_shapes=[
            pltpu.VMEM(wo.shape, BF), pltpu.VMEM((2 * sub, wo.shape[0]), BF),
            pltpu.VMEM((2, nt, 2, sub, tile), F32), pltpu.VMEM((2 * nb, nt, sub, tile), F32),
            pltpu.VMEM((2 * nb, nt, sub, tile), F32), pltpu.VMEM((nb, nt, sub, tile), F32),
            dma, dma((2, nt)), dma((2 * nb, nt)), dma((nb,)), dma((nb,)),
        ],
        compiler_params=pltpu.CompilerParams(vmem_limit_bytes=VMEM_LIMIT, collective_id=1, has_side_effects=True),
        cost_estimate=pl.CostEstimate(flops=40_000_000_000, bytes_accessed=16_000_000, transcendentals=10_000_000),
        name='attention_out',
    )(q, kvs, x, wo)


def peer_of(c, t, d, tp):
    return {'cp': c ^ (d // tp), 'tp': t ^ (d % tp)}, (c ^ (d // tp)) * tp + (t ^ (d % tp))


def far_side(d):
    return (d >> 1) & 1


def place_of(d):
    return (d >> 2) * 2 + (d & 1)


def up_body(h_ref, tgt_ref, g_ref, u_ref, near_ref, cross_ref, pick, sb, xg, send_sem, recv_sem, *, cp, tp, cap, nf, na, wide):
    step = pl.program_id(0)
    ne = cp * tp
    c = lax.axis_index('cp')
    t = lax.axis_index('tp')

    def remote(d):
        where, _ = peer_of(c, t, d, tp)
        return pltpu.make_async_remote_copy(
            src_ref=sb.at[d], dst_ref=xg.at[far_side(d), pl.ds(place_of(d) * cap, cap)], send_sem=send_sem.at[d],
            recv_sem=recv_sem.at[d], device_id=where, device_id_type=MESH)

    @pl.when(step == 0)
    def _():
        barrier = pltpu.get_barrier_semaphore()
        for d in range(1, ne):
            pl.semaphore_signal(barrier, inc=1, device_id=peer_of(c, t, d, tp)[0], device_id_type=MESH)
        slots = lax.broadcasted_iota(jnp.int32, (cap, h_ref.shape[0]), 0)
        for d in range(ne):
            key = slots + peer_of(c, t, d, tp)[1] * cap
            hit = key == tgt_ref[0:1, :]
            for k in range(1, tgt_ref.shape[0]):
                hit = hit | (key == tgt_ref[k:k + 1, :])
            pick[pl.ds(d * cap, cap)] = jnp.where(hit, 1.0, 0.0).astype(BF)

        @pl.loop(0, h_ref.shape[1] // wide)
        def _(j):
            cols = pl.ds(pl.multiple_of(j * wide, wide), wide)
            p = jnp.dot(pick[...], h_ref[:, cols], preferred_element_type=F32).astype(BF)
            xg[0, pl.ds(0, cap), cols] = p[:cap]
            for d in range(1, ne):
                sb[d, :, cols] = p[d * cap:(d + 1) * cap]

        pl.semaphore_wait(barrier, ne - 1)
        for d in (1, 4, 5, 2, 3, 6, 7):
            remote(d).start()
        for d in (1, 4, 5):
            remote(d).wait_recv()

    @pl.when(step == na)
    def _():
        for d in (2, 3, 6, 7):
            remote(d).wait_recv()

    def hidden(x):
        gg = jnp.dot(x, g_ref[0], preferred_element_type=F32)
        uu = jnp.dot(x, u_ref[0], preferred_element_type=F32)
        return (jax.nn.silu(gg) * uu).astype(BF)

    both = (step >= na) & (step < nf)
    half = ne * cap // 2

    @pl.when(both)
    def _():
        r = hidden(xg[...].reshape(ne * cap, xg.shape[2]))
        near_ref[...] = r[:half]
        cross_ref[...] = r[half:]

    @pl.when(jnp.logical_not(both))
    def _():
        r = hidden(xg[(step >= nf).astype(jnp.int32)])

        @pl.when(step < na)
        def _():
            near_ref[...] = r

        @pl.when(step >= nf)
        def _():
            cross_ref[...] = r

    @pl.when(step == nf + na - 1)
    def _():
        for d in range(1, ne):
            remote(d).wait_send()


def expert_up(h, tgt, wg, wu, cp, tp, cap, tile, na):
    t, hd = h.shape
    ff = wg.shape[2]
    ne = cp * tp
    nf = ff // tile
    half = ne * cap // 2
    weights = lambda j: (0, 0, jnp.where(j < nf, j, j - nf))
    dma = pltpu.SemaphoreType.DMA
    return pl.pallas_call(
        functools.partial(up_body, cp=cp, tp=tp, cap=cap, nf=nf, na=na, wide=512),
        grid=(nf + na,),
        in_specs=[
            pl.BlockSpec((t, hd), lambda j: (0, 0)),
            pl.BlockSpec(tgt.shape, lambda j: (0, 0)),
            pl.BlockSpec((1, hd, tile), weights),
            pl.BlockSpec((1, hd, tile), weights),
        ],
        out_specs=[
            pl.BlockSpec((half, tile), lambda j: (0, jnp.minimum(j, nf - 1))),
            pl.BlockSpec((half, tile), lambda j: (0, jnp.where(j < nf, jnp.maximum(j, na), j - nf))),
        ],
        out_shape=[jax.ShapeDtypeStruct((half, ff), BF)] * 2,
        scratch_shapes=[
            pltpu.VMEM((ne * cap, t), BF), pltpu.VMEM((ne, cap, hd), BF), pltpu.VMEM((2, half, hd), BF),
            dma((ne,)), dma((ne,)),
        ],
        compiler_params=pltpu.CompilerParams(vmem_limit_bytes=VMEM_LIMIT, collective_id=cap + 1, has_side_effects=True),
        cost_estimate=pl.CostEstimate(flops=8 * half * hd * ff, bytes_accessed=8 * hd * ff, transcendentals=2 * half * ff),
        name='expert_up',
    )(h, tgt, wg, wu)


def down_body(near_hbm, cross_hbm, w_ref, h_ref, tgt_ref, gate_ref, y_ref, act, zs, zb, load_sem, send_sem, recv_sem, own_sem,
              *, cp, tp, cap, nt, lag):
    step = pl.program_id(0)
    ne = cp * tp
    c = lax.axis_index('cp')
    t = lax.axis_index('tp')
    me = c * tp + t

    def mine():
        return pl.ds(pl.multiple_of(me * cap, cap), cap)

    def theirs(d):
        return pl.ds((far_side(d) * ne // 2 + place_of(d)) * cap, cap)

    def remote(n, d):
        where, _ = peer_of(c, t, d, tp)
        return pltpu.make_async_remote_copy(
            src_ref=zs.at[n, theirs(d)], dst_ref=zb.at[n, mine()], send_sem=send_sem.at[n, d],
            recv_sem=recv_sem.at[n, d], device_id=where, device_id_type=MESH)

    def own(n):
        return pltpu.make_async_copy(zs.at[n, theirs(0)], zb.at[n, mine()], own_sem.at[n])

    @pl.when(step == 0)
    def _():
        half = ne * cap // 2
        loads = [pltpu.make_async_copy(near_hbm, act.at[pl.ds(0, half)], load_sem.at[0]),
                 pltpu.make_async_copy(cross_hbm, act.at[pl.ds(half, half)], load_sem.at[1])]
        for ld in loads:
            ld.start()
        barrier = pltpu.get_barrier_semaphore()
        for d in range(1, ne):
            pl.semaphore_signal(barrier, inc=1, device_id=peer_of(c, t, d, tp)[0], device_id_type=MESH)
        pl.semaphore_wait(barrier, ne - 1)
        for ld in loads:
            ld.wait()

    @pl.when((step >= 1) & (step <= nt))
    def _():
        for d in (2, 3, 6, 7, 4, 5, 1):
            remote(step - 1, d).start()
        own(step - 1).start()

    @pl.when(step < nt)
    def _():
        zs[step] = jnp.dot(act[...], w_ref[0], preferred_element_type=F32).astype(BF)

    @pl.when(step >= lag)
    def _():
        n = step - lag
        own(n).wait()
        for d in range(1, ne):
            remote(n, d).wait_recv()
        slots = lax.broadcasted_iota(jnp.int32, (tgt_ref.shape[0], ne * cap), 1)
        z = zb[n]
        acc = h_ref[...].astype(F32)
        zsum = None
        for k in range(tgt_ref.shape[1]):
            pick = (slots == tgt_ref[:, k:k + 1]).astype(BF)
            zk = gate_ref[:, k:k + 1] * jnp.dot(pick, z, preferred_element_type=F32)
            zsum = zk if zsum is None else zsum + zk
        y_ref[...] = (acc + zsum).astype(BF)
        for d in range(1, ne):
            remote(n, d).wait_send()


def expert_down(near, cross, wd, h, tgt, gates, cp, tp, cap, tile, lag):
    half, ff = near.shape
    r = 2 * half
    t, hd = h.shape
    kk = tgt.shape[1]
    ne = cp * tp
    nt = hd // tile
    late = lambda j: (0, jnp.maximum(j - lag, 0))
    dma = pltpu.SemaphoreType.DMA
    return pl.pallas_call(
        functools.partial(down_body, cp=cp, tp=tp, cap=cap, nt=nt, lag=lag),
        grid=(nt + lag,),
        in_specs=[
            pl.BlockSpec(memory_space=pl.ANY),
            pl.BlockSpec(memory_space=pl.ANY),
            pl.BlockSpec((1, ff, tile), lambda j: (0, 0, jnp.minimum(j, nt - 1))),
            pl.BlockSpec((t, tile), late),
            pl.BlockSpec((t, kk), lambda j: (0, 0)),
            pl.BlockSpec((t, kk), lambda j: (0, 0)),
        ],
        out_specs=pl.BlockSpec((t, tile), late),
        out_shape=jax.ShapeDtypeStruct((t, hd), BF),
        scratch_shapes=[
            pltpu.VMEM((r, ff), BF),
            pltpu.VMEM((nt, r, tile), BF),
            pltpu.VMEM((nt, r, tile), BF),
            dma((2,)), dma((nt, ne)), dma((nt, ne)), dma((nt,)),
        ],
        compiler_params=pltpu.CompilerParams(vmem_limit_bytes=VMEM_LIMIT, collective_id=cap, has_side_effects=True),
        cost_estimate=pl.CostEstimate(flops=2 * r * hd * ff, bytes_accessed=2 * hd * ff, transcendentals=0),
        name='expert_down',
    )(near, cross, wd, h, tgt, gates)


def solution(mesh):
    cp = mesh.shape['cp']
    tp = mesh.shape['tp']
    ne = cp * tp
    rows_spec = P(('dp', 'cp', 'tp'), None)
    exp_spec = P(('cp', 'tp'), None, None)

    def local(x, idx, gates, wq, wk, wv, wo, w1g, w1u, w2):
        t, hd = x.shape
        kk = idx.shape[1]

        ea = idx.reshape(-1)
        onehot = (ea[:, None] == jnp.arange(ne)[None, :]).astype(jnp.int32)
        cum = jnp.cumsum(onehot, axis=0)
        slot = (jnp.sum(cum * onehot, axis=1) - 1).reshape(t, kk)
        cnt = jnp.broadcast_to(jnp.max(cum[-1]), (8, 128))
        q, kvs, top = project_qkv(x, cnt, wq, wk, wv, cp, tp)
        fullest = top[0, 0]
        h = attention_out(q, kvs, x, wo, cp, tp)

        def moe(cap):
            def run(h, idx, slot, gates, w1g, w1u, w2):
                tgt = idx * cap + slot
                near, cross = expert_up(h, tgt.T, w1g, w1u, cp, tp, cap, 256, 16)
                return expert_down(near, cross, w2, h, tgt, gates, cp, tp, cap, 256, 4)
            return run

        caps = (2 * t // ne, 3 * t // ne, 4 * t // ne)
        tier = (fullest > caps[0]).astype(jnp.int32) + (fullest > caps[1]).astype(jnp.int32)
        return lax.switch(tier, [moe(cap) for cap in caps], h, idx, slot, gates, w1g, w1u, w2)

    return jax.shard_map(local, mesh=mesh, in_specs=(rows_spec, rows_spec, rows_spec, P(None, 'tp'), P(None, 'tp'), P(None, 'tp'), P('tp', None), exp_spec, exp_spec, exp_spec), out_specs=rows_spec, check_vma=False)
```

time: 634 us -> 505 us (0.80)
  waiting for transfers between devices: 250 us -> 0 us
  Pallas kernels: 265 us -> 493 us
  matrix products: 42.9 us -> 0 us
  blocking collectives: 22.9 us -> 0 us
  starting transfers between devices: 15.6 us -> 0 us
  between operations: 15 us -> 1.38 us
    pallas_call x3 -> x4, Pallas kernels: 265 us -> 493 us  [the longest x1 180 us: expert_up(): pl.pallas_call(functools.partial(up_body, cp=cp, tp=tp, cap=cap, nf=nf, n...]
    all_to_all x1 -> x0, waiting for transfers between devices: 93.2 us -> none  [run(): recv = lax.all_to_all(send, ('cp', 'tp'), 0, 0, tiled=True)]
    reduce_scatter x1 -> x0, waiting for transfers between devices: 92 us -> none  [local(): att = lax.psum_scatter(part, 'tp', scatter_dimension=0, tiled=True)]
    all_gather x2 -> x0, waiting for transfers between devices: 64.2 us -> none  [the longest x1 60.1 us: local(): xs = lax.all_gather(x, 'tp', axis=0, tiled=True)]
    dot_general x5 -> x0, matrix products: 42.9 us -> none  [the longest x1 14.6 us: local(): q = jnp.dot(xs, wq, preferred_element_type=F32).astype(BF)]
    pmax x1 -> x0, blocking collectives: 22.9 us -> none  [local(): fullest = lax.pmax(jnp.max(cum[-1]), ('cp', 'tp'))]
    reduce_scatter x1 -> x0, starting transfers between devices: 11.6 us -> none  [local(): att = lax.psum_scatter(part, 'tp', scatter_dimension=0, tiled=True)]
  transfers between devices with their start and end apart: 4 -> 0, of which waited for: 4 -> 0; matrix products, arithmetic and copies ran while one was open for 3% -> 0% of each run, Pallas kernels for 0% -> 0%
where the time goes in v2:
time: 505 us; the launch traced here: 504 us
  Pallas kernels  493 us (98%)
  local copies, waits for them, and re-layouts  7.18 us (1%)
    pallas_call x1, Pallas kernels, expert_up(): pl.pallas_call(functools.partial(up_body, cp=cp, tp=tp, cap=cap, nf=nf, n...  180 us
    pallas_call x1, Pallas kernels, expert_down(): pl.pallas_call(functools.partial(down_body, cp=cp, tp=tp, cap=cap, nt=nt,...  146 us
    pallas_call x1, Pallas kernels, attention_out(): pl.pallas_call(functools.partial(attn_out_body, cp=cp, tp=tp, nb=nb, tile...  105 us
    pallas_call x1, Pallas kernels, project_qkv(): pl.pallas_call(functools.partial(qkv_body, cp=cp, tp=tp, ch=ch), in_specs...  61.2 us

profile of v2, /device:TPU:0, one launch (start us, length us, event | category | flops | bytes accessed | tf_op | source)
XLA Modules:
  0.0 504.3 jit_solution(4550899211790324528)
XLA Ops:
  0.0 0.8 copy.53
  0.8 0.1 eq.25
  1.0 1.1 reduce-window.6
  2.1 0.2 slice_reduce_fusion
  2.4 0.1 add_bitcast_fusion
  2.5 0.8 slice_reduce_fusion.1
  3.3 1.3 broadcast_in_dim.4.cnt_ref
  4.5 61.2 %project_qkv.1 = (bf16[1024,1024]{1,0:T(8,128)(2,1)}, bf16[2,1024,512]{2,1,0:T(8,128)(2,1)}, s32[8,128]{1,0:T(8,128)}) custom-call(bf16[256,4096]{1,0:T(8,128)(2,1)} %x_ref.3, s32[8,128]{1,0:T(8,128)} %broadcast_in_dim.4.cnt_ref, bf16[4096,1024]{1,0:T(8,128)(2,1)} %wq_hbm.1, bf16[4096,256]{1,0:T(8,128)(2,1)} %wk_hbm.1, bf16[4096,256]{1,0:T(8,128)(2,1)} %wv_hbm.1), custom_call_target="tpu_custom_call" | custom-call | flops 12884901888 | bytes 20000000 | tf_op jit(solution)/shard_map/project_qkv/pallas_call | solution.py:129
  65.8 1.2 slice.15
  68.3 0.0 copy-start.3
  68.3 0.0 copy-start.4
  68.3 105.3 %attention_out.1 = bf16[256,4096]{1,0:T(8,128)(2,1)S(1)} custom-call(bf16[1024,1024]{1,0:T(8,128)(2,1)} %get-tuple-element.82.q_ref, bf16[2,1024,512]{2,1,0:T(8,128)(2,1)} %get-tuple-element.83.kv_ref, bf16[256,4096]{1,0:T(8,128)(2,1)} %x_ref.3, bf16[1024,4096]{1,0:T(8,128)(2,1)} %wo_hbm.1), custom_call_target="tpu_custom_call" | custom-call | flops 40000000000 | bytes 16000000 | tf_op jit(solution)/shard_map/attention_out/pallas_call | solution.py:290
  173.6 0.0 copy-done.3
  173.6 0.0 copy-done.4
  173.6 329.3 %conditional.1 = (bf16[256,4096]{1,0:T(8,128)(2,1)S(1)}) conditional(s32[]{:T(128)} %bitcast.2, (s32[256,2]{0,1:T(2,128)S(1)}, s32[256,2]{0,1:T(2,128)S(1)}, bf16[256,4096]{1,0:T(8,128)(2,1)S(1)}, bf16[1,4096,6400]{2,1,0:T(8,128)(2,1)}, bf16[1,4096,6400]{2,1,0:T(8,128)(2,1)}, ...), branch_computations={%region_4.5_spmd.clone, %region_5.6_spmd.clone, %region_6.7_spmd.c... | conditional | flops 161061289984 | bytes 270612544 | solution.py:556
  173.9 0.0 copy-start.7
  174.0 1.0 copy.62.gate_ref
  174.9 0.1 copy.61
  175.1 0.1 eq.50
  175.2 0.1 sub.18
  175.4 0.1 copy.60
  175.6 0.0 copy-start.2
  175.6 0.7 copy.52.tgt_ref
  176.2 180.1 %expert_up.5 = (bf16[512,6400]{1,0:T(8,128)(2,1)}, bf16[512,6400]{1,0:T(8,128)(2,1)}) custom-call(bf16[256,4096]{1,0:T(8,128)(2,1)S(1)} %get-tuple-element.199.h_ref, s32[2,256]{1,0:T(2,128)} %copy.52.tgt_ref, bf16[1,4096,6400]{2,1,0:T(8,128)(2,1)} %get-tuple-element.203.g_ref, bf16[1,4096,6400]{2,1,0:T(8,128)(2,1)} %get-tuple-element.204.u_ref), custom_call_target="tpu_custom_call" | custom-call | flops 107374182400 | bytes 209715200 | tf_op jit(solution)/shard_map/cond/branch_2_fun/expert_up/pallas_call | solution.py:403
  356.3 0.0 copy-done.7
  356.3 0.0 copy-done.2
  356.3 146.3 %expert_down.5 = bf16[256,4096]{1,0:T(8,128)(2,1)S(1)} custom-call(bf16[512,6400]{1,0:T(8,128)(2,1)} %get-tuple-element.201.near_hbm, bf16[512,6400]{1,0:T(8,128)(2,1)} %get-tuple-element.202.cross_hbm, bf16[1,6400,4096]{2,1,0:T(8,128)(2,1)} %get-tuple-element.205.w_ref, bf16[256,4096]{1,0:T(8,128)(2,1)} %copy-done.7, s32[256,2]{1,0:T(8,128)} %copy-done.2, ...), custom_call_target="tpu_custom_call" | custom-call | flops 53687091200 | bytes 52428800 | tf_op jit(solution)/shard_map/cond/branch_2_fun/expert_down/pallas_call | solution.py:502
  503.0 1.3 copy.67
  (7 shorter events, 0.1 us)
Async XLA Ops:
  68.3 105.4 %copy-start.3 = (s32[256,2]{0,1:T(2,128)S(1)}, s32[256,2]{0,1:T(2,128)}, u32[]{:S(2)}) copy-start(s32[256,2]{0,1:T(2,128)} %param.14) | copy-start | bytes 6148
  68.3 105.4 %copy-start.4 = (f32[256,2]{0,1:T(2,128)S(1)}, f32[256,2]{0,1:T(2,128)}, u32[]{:S(2)}) copy-start(f32[256,2]{0,1:T(2,128)} %param.15) | copy-start | bytes 6148
  173.9 182.4 %copy-start.7 = (bf16[256,4096]{1,0:T(8,128)(2,1)}, bf16[256,4096]{1,0:T(8,128)(2,1)S(1)}, u32[]{:S(2)}) copy-start(bf16[256,4096]{1,0:T(8,128)(2,1)S(1)} %get-tuple-element.199.h_ref) | copy-start | bytes 6291460 | tf_op jit(solution)/shard_map/cond
  175.6 180.8 %copy-start.2 = (s32[256,2]{1,0:T(8,128)}, s32[256,2]{1,0:T(8,128)S(1)}, u32[]{:S(2)}) copy-start(s32[256,2]{1,0:T(8,128)S(1)} %multiply_add_fusion.2.tgt_ref) | copy-start | bytes 6148 | tf_op jit(solution)/shard_map/cond
